TPU v7x, 32 devices: a whole 2x2x4 slice. The times are simulated.
32 devices in a mesh: row: 8 (over y, x, core), col: 4 (over z).
Axes of the slice: x: 2, y: 2, z: 4, core: 2. Of those that a mesh axis runs over, the one named last changes fastest.
Arguments:
- window_rows: bfloat16 [1024, 65536], P('row', 'col'), may hold values from -6 to 6
- omega_cols: bfloat16 [512, 1024], P(None, 'row'), may hold values from -0.1875 to 0.1875
- psi_rows: bfloat16 [65536, 1024], P(('col', 'row')), may hold values from -0.046875 to 0.046875
- upsilon_rows: bfloat16 [65536, 2048], P(('col', 'row')), may hold values from -0.046875 to 0.046875
- phi_cols: bfloat16 [2048, 1024], P(None, 'row'), may hold values from -0.1875 to 0.1875
- range_old: float32 [512, 65536], P(None, ('col', 'row')), may hold values from -6 to 6
- core_old: float32 [2048, 2048], P('row', 'col'), may hold values from -6 to 6
Outputs:
- range_sketch: float32 [512, 65536], P(None, ('col', 'row'))
- corange_sketch: float32 [1024, 1024], P('row', 'col')
- core_sketch: float32 [2048, 2048], P('row', 'col')
All inputs are finite; a program needn't handle non-finite values.
Results may differ from a plain program's by a relative error of at most 0.0022.
Values may be sent and summed in bfloat16 or wider, within the bound.
A program may use at most 128 MiB of HBM per device.

v0:
```python
import functools

import jax
import jax.numpy as jnp
from jax import lax
from jax.experimental import pallas as pl
from jax.experimental.pallas import tpu as pltpu
from jax.sharding import PartitionSpec as P

MESH = pl.DeviceIdType.MESH
LIMIT = 60 * 1024 * 1024


def greet(peers):
    barrier = pltpu.get_barrier_semaphore()
    for peer in peers:
        pl.semaphore_signal(barrier, inc=1, device_id=peer, device_id_type=MESH)
    pl.semaphore_wait(barrier, len(peers))


def send(src, dst, send_sem, recv_sem, peer):
    copy = pltpu.make_async_remote_copy(
        src_ref=src, dst_ref=dst, send_sem=send_sem, recv_sem=recv_sem, device_id=peer, device_id_type=MESH
    )
    copy.start()
    return copy


def exchange(n, window, phi, relaid, phi_all, keep_w, keep_p, send_sem, recv_sem, local_sem):
    me = lax.axis_index("row")
    rows, width = window.shape[0], relaid.shape[1]
    core_rows, depth = phi_all.shape[0], phi.shape[1]
    peers = [lax.rem(me + d, n) for d in range(1, n)]
    greet([{"row": p} for p in peers])
    copies = []
    for d, p in enumerate(peers):
        copies.append(send(
            window.at[:, pl.ds(pl.multiple_of(p * width, width), width)],
            relaid.at[pl.ds(pl.multiple_of(me * rows, rows), rows), :],
            send_sem.at[0, d], recv_sem.at[0, d], {"row": p}))
    for d, p in enumerate(peers):
        copies.append(send(
            phi.at[pl.ds(pl.multiple_of(p * core_rows, core_rows), core_rows), :],
            phi_all.at[:, pl.ds(pl.multiple_of(me * depth, depth), depth)],
            send_sem.at[1, d], recv_sem.at[1, d], {"row": p}))
    ins = (
        pltpu.make_async_copy(window.at[:, pl.ds(pl.multiple_of(me * width, width), width)], keep_w, local_sem.at[0]),
        pltpu.make_async_copy(phi.at[pl.ds(pl.multiple_of(me * core_rows, core_rows), core_rows), :], keep_p, local_sem.at[1]),
    )
    for c in ins:
        c.start()
    for c in ins:
        c.wait()
    outs = (
        pltpu.make_async_copy(keep_w, relaid.at[pl.ds(pl.multiple_of(me * rows, rows), rows), :], local_sem.at[2]),
        pltpu.make_async_copy(keep_p, phi_all.at[:, pl.ds(pl.multiple_of(me * depth, depth), depth)], local_sem.at[3]),
    )
    for c in outs:
        c.start()
    for c in outs:
        c.wait()
    for c in copies:
        c.wait()


def reduce_kernel(n, m, sk, co, gathered, co_out, *scratch):
    (acc_sk, acc_co, *recv), rest = scratch[:2 + 2 * (n.bit_length() - 1)], scratch[2 + 2 * (n.bit_length() - 1):]
    fin_sk, fin_co, z_sk, z_co, mine, load_sem, ss, rs, zs, zr, gs, gr, ls = rest
    levels = n.bit_length() - 1
    me, c = lax.axis_index("row"), lax.axis_index("col")
    bits = [(me // (1 << b)) % 2 for b in range(levels)]
    partner = [{"row": me + (1 - 2 * bits[b]) * (1 << b)} for b in range(levels)]
    row_peers = [lax.rem(me + d, n) for d in range(1, n)]
    col_peers = [lax.rem(c + d, m) for d in range(1, m)]
    greet([{"row": p} for p in row_peers] + [{"col": p} for p in col_peers])

    pieces = []
    low, high = list(range(1, levels)), list(range(levels - 1, 0, -1))
    for k, (src, acc, fin) in enumerate(((sk, acc_sk, fin_sk), (co, acc_co, fin_co))):
        half = src.shape[-1] // 2
        for h, order in enumerate((low, high)):
            pieces.append((src, acc, recv[k::2], fin, pl.ds(h * half, half), order))

    copies = []
    first = []
    for q, (src, acc, got, fin, cols, order) in enumerate(pieces):
        first.append([
            send(src.at[i, 1 - bits[0], :, cols], got[0].at[i, :, cols], ss.at[q, 0, i], rs.at[q, 0, i], partner[0])
            for i in range(n // 2)])
    loads = []
    for q, (src, acc, got, fin, cols, order) in enumerate(pieces):
        load = pltpu.make_async_copy(src.at[:, bits[0], :, cols], acc.at[:, :, cols], load_sem.at[q])
        load.start()
        loads.append(load)

    live = [(0, n // 2, 1)] * 4
    started = [None] * 4

    def pair(q):
        src, acc, got, fin, cols, order = pieces[q]
        loads[q].wait()
        for i in range(n // 2):
            first[q][i].wait_recv()
            acc[i, :, cols] += got[0][i, :, cols]
        copies.extend(first[q])

    def give(q, step):
        src, acc, got, fin, cols, order = pieces[q]
        base, count, stride = live[q]
        bit, half = bits[order[step]], count // 2
        if order is low:
            live[q] = (base + stride * bit, half, stride * 2)
            start, jump = base + stride * (1 - bit), stride * 2
        else:
            live[q] = (base + stride * half * bit, half, stride)
            start, jump = base + stride * half * (1 - bit), stride
        started[q] = [
            send(acc.at[start + jump * i, :, cols], got[step + 1].at[i, :, cols],
                 ss.at[q, step + 1, i], rs.at[q, step + 1, i], partner[order[step]])
            for i in range(half)]

    def take(q, step):
        src, acc, got, fin, cols, order = pieces[q]
        base, count, stride = live[q]
        for i in range(count):
            started[q][i].wait_recv()
            if step == levels - 2:
                fin[:, cols] = acc[base + stride * i, :, cols] + got[step + 1][i, :, cols]
            else:
                acc[base + stride * i, :, cols] += got[step + 1][i, :, cols]
        copies.extend(started[q])

    def cross(k):
        fin, z = ((fin_sk, z_sk), (fin_co, z_co))[k]
        width = z.shape[-1]
        return [
            send(fin.at[:, pl.ds(pl.multiple_of(p * width, width), width)], z.at[d], zs.at[k, d], zr.at[k, d], {"col": p})
            for d, p in enumerate(col_peers)]

    for q in (0, 1):
        pair(q)
        give(q, 0)
    for q in (2, 3):
        pair(q)
    for step in range(levels - 1):
        for q in (0, 1):
            take(q, step)
            if step < levels - 2:
                give(q, step + 1)
        if step == max(levels - 3, 0):
            for q in (2, 3):
                give(q, 0)
    across = [cross(0)]
    for step in range(levels - 1):
        for q in (2, 3):
            take(q, step)
            if step < levels - 2:
                give(q, step + 1)
    across.append(cross(1))
    for k, (fin, z) in enumerate(((fin_sk, z_sk), (fin_co, z_co))):
        width = z.shape[-1]
        own = pl.ds(pl.multiple_of(c * width, width), width)
        for copy in across[k]:
            copy.wait_recv()
        total = fin[:, own]
        for d in range(m - 1):
            total = total + z[d]
        if k == 0:
            mine[...] = total.astype(mine.dtype)
            rows = mine.shape[0]
            place = gathered.at[pl.ds(pl.multiple_of(me * rows, rows), rows), :]
            spread = [
                send(mine, place, gs.at[d], gr.at[d], {"row": p}) for d, p in enumerate(row_peers)]
            put = pltpu.make_async_copy(mine, place, ls)
            put.start()
        else:
            co_out[...] = total
        copies += across[k]
    put.wait()
    for copy in spread:
        copy.wait()
    for copy in copies:
        copy.wait_send()


def shards(n, m, window_rows, omega_cols, psi_rows, upsilon_rows, phi_cols, range_old, core_old):
    any_space = pl.BlockSpec(memory_space=pl.ANY)
    vmem = pl.BlockSpec(memory_space=pltpu.VMEM)
    dma = pltpu.SemaphoreType.DMA
    rows, wide = window_rows.shape
    own = wide // n
    core_rows = phi_cols.shape[0] // n
    bf16, f32 = jnp.bfloat16, jnp.float32
    relaid, phi_all = pl.pallas_call(
        functools.partial(exchange, n),
        out_shape=(jax.ShapeDtypeStruct((rows * n, own), bf16), jax.ShapeDtypeStruct((core_rows, rows * n), bf16)),
        in_specs=[any_space] * 2,
        out_specs=(any_space, any_space),
        scratch_shapes=[
            pltpu.VMEM((rows, own), bf16), pltpu.VMEM((core_rows, rows), bf16),
            dma((2, n - 1)), dma((2, n - 1)), dma((4,)),
        ],
        compiler_params=pltpu.CompilerParams(collective_id=0, has_side_effects=True),
        name="exchange",
    )(window_rows, phi_cols)
    relaid, omega_cols = lax.optimization_barrier((relaid, omega_cols))
    omega = lax.all_gather(omega_cols, "row", axis=1, tiled=True)
    core_part = jnp.dot(relaid, upsilon_rows, preferred_element_type=f32)
    co_part = jnp.dot(relaid, psi_rows, preferred_element_type=f32)
    s, l = core_part.shape[1], co_part.shape[1]
    levels = n.bit_length() - 1
    scratch = [pltpu.VMEM((n // 2, rows, s), f32), pltpu.VMEM((n // 2, rows, l), f32)]
    for b in range(levels):
        scratch += [pltpu.VMEM((n >> (b + 1), rows, s), f32), pltpu.VMEM((n >> (b + 1), rows, l), f32)]
    scratch += [
        pltpu.VMEM((rows, s), f32), pltpu.VMEM((rows, l), f32),
        pltpu.VMEM((m - 1, rows, s // m), f32), pltpu.VMEM((m - 1, rows, l // m), f32),
        pltpu.VMEM((rows, s // m), bf16), dma((4,)),
        dma((4, levels, n // 2)), dma((4, levels, n // 2)),
        dma((2, m - 1)), dma((2, m - 1)), dma((n - 1,)), dma((n - 1,)), dma,
    ]
    gathered, corange_sketch = pl.pallas_call(
        functools.partial(reduce_kernel, n, m),
        out_shape=(jax.ShapeDtypeStruct((rows * n, s // m), bf16), jax.ShapeDtypeStruct((rows, l // m), f32)),
        in_specs=[any_space] * 2,
        out_specs=(any_space, vmem),
        scratch_shapes=scratch,
        compiler_params=pltpu.CompilerParams(collective_id=1, has_side_effects=True, vmem_limit_bytes=LIMIT),
        name="reduce",
    )(core_part.reshape(n // 2, 2, rows, s), co_part.reshape(n // 2, 2, rows, l))
    range_sketch = range_old + jnp.dot(omega, relaid, preferred_element_type=f32)
    core_sketch = core_old + jnp.dot(phi_all, gathered, preferred_element_type=f32)
    return (range_sketch, corange_sketch, core_sketch)


def solution(mesh):
    placed = (
        P("row", "col"),
        P(None, "row"),
        P(("col", "row"), None),
        P(("col", "row"), None),
        P(None, "row"),
        P(None, ("col", "row")),
        P("row", "col"),
    )
    return jax.shard_map(
        functools.partial(shards, mesh.shape["row"], mesh.shape["col"]),
        mesh=mesh,
        in_specs=placed,
        out_specs=(P(None, ("col", "row")), P("row", "col"), P("row", "col")),
        check_vma=False,
    )
```

profile of v0, /device:TPU:11, one launch (start us, length us, event | category | flops | bytes accessed | tf_op | source)
XLA Modules:
  0.0 191.5 jit_solution(16615213677621380337)
XLA Ops:
  7.2 0.0 all-gather.2.cloned.1.call-start
  7.2 55.2 %exchange.1 = (bf16[1024,2048]{1,0:T(8,128)(2,1)}, bf16[256,1024]{1,0:T(8,128)(2,1)}) custom-call(bf16[128,16384]{1,0:T(8,128)(2,1)} %window.1, bf16[2048,128]{1,0:T(8,128)(2,1)} %phi.1), custom_call_target="tpu_custom_call" | custom-call | tf_op jit(solution)/shard_map/exchange/pallas_call | solution.py:194
  62.4 0.0 all-gather.2.cloned.1.call-update
  62.5 0.0 copy-start.3
  62.5 0.0 copy-start.4
  62.5 10.1 %fusion.1 = f32[1024,1024]{1,0:T(8,128)} fusion(bf16[1024,2048]{1,0:T(8,128)(2,1)} %get-tuple-element.11, bf16[2048,1024]{1,0:T(8,128)(2,1)} %param.9), kind=kOutput, calls=%fused_computation.3 | convolution fusion | flops 4294967296 | bytes 12582912 | tf_op jit(solution)/shard_map/dot_general | solution.py:209
  72.6 0.0 copy-done.3
  72.6 0.0 copy-done.4
  72.6 11.0 %fusion = f32[1024,2048]{1,0:T(8,128)} fusion(bf16[1024,2048]{1,0:T(8,128)(2,1)S(1)} %copy-done.4, bf16[2048,2048]{1,0:T(8,128)(2,1)S(1)} %copy-done.3), kind=kOutput, calls=%fused_computation.2 | convolution fusion | flops 8589934592 | bytes 20971520 | tf_op jit(solution)/shard_map/dot_general | solution.py:208
  83.6 0.0 copy-start
  83.6 0.0 copy-start.1
  83.6 89.7 %reduce.1 = (bf16[1024,512]{1,0:T(8,128)(2,1)}, f32[128,256]{1,0:T(8,128)}) custom-call(f32[4,2,128,2048]{3,2,1,0:T(8,128)} %bitcast.10, f32[4,2,128,1024]{3,2,1,0:T(8,128)} %bitcast.11), custom_call_target="tpu_custom_call" | custom-call | tf_op jit(solution)/shard_map/reduce/pallas_call | solution.py:222
  173.3 0.0 copy-done
  173.3 0.0 copy-done.1
  173.3 2.5 %convolution_add_fusion.1 = f32[256,512]{1,0:T(8,128)} fusion(f32[256,512]{1,0:T(8,128)S(1)} %copy-done, bf16[256,1024]{1,0:T(8,128)(2,1)S(1)} %copy-done.1, bf16[1024,512]{1,0:T(8,128)(2,1)} %get-tuple-element.14), kind=kOutput, calls=%fused_computation.1 | convolution fusion | flops 268566528 | bytes 2621440 | tf_op jit(solution)/shard_map/dot_general | solution.py:232
  175.8 0.0 copy-start.2
  175.8 0.0 all-gather.2.cloned.1.call-done
  175.8 8.2 %convolution_add_fusion = f32[512,2048]{1,0:T(8,128)} fusion(f32[512,2048]{1,0:T(8,128)} %param.12, bf16[512,1024]{1,0:T(8,128)(2,1)} %all-gather.2.cloned.1.call-done, bf16[1024,2048]{1,0:T(8,128)(2,1)} %get-tuple-element.11), kind=kOutput, calls=%fused_computation | convolution fusion | flops 2148532224 | bytes 13631488 | tf_op jit(solution)/shard_map/dot_general | solution.py:231
  184.0 0.0 copy-done.2
  184.0 0.7 copy.11
Async XLA Ops:
  7.2 168.6 %all-gather.2.cloned.1.call-start = ((), (), s32[]{:S(2)}) async-start(), calls=%async_computation | async-start | bytes 1179648 | tf_op jit(solution)/shard_map/all_gather | solution.py:207
  62.5 10.1 %copy-start.3 = (bf16[2048,2048]{1,0:T(8,128)(2,1)S(1)}, bf16[2048,2048]{1,0:T(8,128)(2,1)}, u32[]{:S(2)}) copy-start(bf16[2048,2048]{1,0:T(8,128)(2,1)} %param.10) | copy-start | bytes 25165828
  62.5 10.1 %copy-start.4 = (bf16[1024,2048]{1,0:T(8,128)(2,1)S(1)}, bf16[1024,2048]{1,0:T(8,128)(2,1)}, u32[]{:S(2)}) copy-start(bf16[1024,2048]{1,0:T(8,128)(2,1)} %get-tuple-element.11) | copy-start | bytes 12582916
  83.6 89.8 %copy-start = (f32[256,512]{1,0:T(8,128)S(1)}, f32[256,512]{1,0:T(8,128)}, u32[]{:S(2)}) copy-start(f32[256,512]{1,0:T(8,128)} %param.13) | copy-start | bytes 1572868
  83.6 89.8 %copy-start.1 = (bf16[256,1024]{1,0:T(8,128)(2,1)S(1)}, bf16[256,1024]{1,0:T(8,128)(2,1)}, u32[]{:S(2)}) copy-start(bf16[256,1024]{1,0:T(8,128)(2,1)} %get-tuple-element.13) | copy-start | bytes 1572868
  175.8 8.2 %copy-start.2 = (f32[128,256]{1,0:T(8,128)S(1)}, f32[128,256]{1,0:T(8,128)}, u32[]{:S(2)}) copy-start(f32[128,256]{1,0:T(8,128)} %get-tuple-element.19) | copy-start | bytes 393220
Sparse Core Ops, SparseCore 0:
  62.6 24.4 all-gather.1
where the time goes:
time: 192 us; the launch traced here: 191 us
  Pallas kernels  145 us (76%)
  matrix products  31.7 us (17%)
  between operations  14.1 us (7%)
    pallas_call x1, Pallas kernels, shards(): pl.pallas_call(functools.partial(reduce_kernel, n, m), out_shape=(jax.Sha...  89.7 us
    pallas_call x1, Pallas kernels, shards(): pl.pallas_call(functools.partial(exchange, n), out_shape=(jax.ShapeDtypeS...  55.2 us
    dot_general x1, matrix products, shards(): core_part = jnp.dot(relaid, upsilon_rows, preferred_element_type=f32)  11 us
    dot_general x1, matrix products, shards(): co_part = jnp.dot(relaid, psi_rows, preferred_element_type=f32)  10.1 us
    dot_general x1, matrix products, shards(): jnp.dot(omega, relaid, preferred_element_type=f32)  8.16 us
  transfers between devices with their start and end apart: 1, of which 0 were waited for; matrix products, arithmetic and copies ran while one was open for 12% of the time, Pallas kernels for 47%

commit v1 on v0

v1 whole, which is shorter than its diff:
```python
import functools

import jax
import jax.numpy as jnp
from jax import lax
from jax.experimental import pallas as pl
from jax.experimental.pallas import tpu as pltpu
from jax.sharding import PartitionSpec as P

MESH = pl.DeviceIdType.MESH
LIMIT = 63 * 1024 * 1024
F32, BF16 = jnp.float32, jnp.bfloat16


def encode(x):
    return (x * jnp.abs(x)).astype(BF16)


def decode(y):
    y = y.astype(F32)
    return y * lax.rsqrt(jnp.maximum(jnp.abs(y), 1e-37))


def flip(index, mask, count):
    total, bit = 0, 1
    while bit < count:
        own = (index // bit) % 2
        total = total + (1 - own if mask & bit else own) * bit
        bit *= 2
    return total


def piece_order(chips):
    classes = {}
    for o in range(chips):
        classes.setdefault(bin(o).count("1"), []).append(o)
    return [(o, h) for k in sorted(classes) for h in range(2) for o in classes[k]]


def sketch_kernel(n, m, window, omega, psi, ups, phi, range_old, core_old, range_out, co_out, core_out,
                  relaid, psi_v, ups_v, xs, xr, keep, zs, z1r, z2r, own, ys, yr, gathered, phi_all, omega_all, range_v,
                  w_sem, l_sem, a_s, a_r, p_s, p_r, x_s, x_r, z_s, z1_s, z2_s, y_s, y_r, g_s, g_r, f_s, f_r, r_sem):
    me, c = lax.axis_index("row"), lax.axis_index("col")
    chips = n // 2
    rows, width = window.shape[0], relaid.shape[1]
    half = rows // 2
    lz = psi_v.shape[1] // m
    sz = ups_v.shape[1] // m
    cz = lz + sz
    slots = keep.shape[0]
    core_rows, depth = phi_all.shape[0], phi.shape[1]
    pieces = piece_order(chips)
    odd = c % 2
    side = c + odd * (m - 1 - 2 * c)
    first = m - 1 - side
    near = c + 1 - 2 * odd
    pair = c // 2

    def at(r, h):
        return pl.ds(pl.multiple_of(r * rows + h * half, half), half)

    def block(r, size):
        return pl.ds(pl.multiple_of(r * size, size), size)

    def peer(mask):
        return flip(me, mask, n)

    def chunk(t):
        ahead = jnp.where(t < first, m - 1 - t, jnp.where(t < m - 1, t - first, side))
        return ahead + odd * (m - 1 - 2 * ahead)

    def remote(src, dst, send_sem, recv_sem, device):
        return pltpu.make_async_remote_copy(
            src_ref=src, dst_ref=dst, send_sem=send_sem, recv_sem=recv_sem, device_id=device, device_id_type=MESH)

    def weights(d):
        return (
            pltpu.make_async_copy(psi.at[:, block(d, lz)], psi_v.at[:, block(d, lz)], w_sem.at[d, 0]),
            pltpu.make_async_copy(ups.at[:, block(d, sz)], ups_v.at[:, block(d, sz)], w_sem.at[d, 1]))

    local = [
        pltpu.make_async_copy(window.at[pl.ds(h * half, half), block(me, width)], relaid.at[at(me, h), :], l_sem.at[h])
        for h in range(2)]
    local += [
        pltpu.make_async_copy(phi.at[block(me, core_rows), :], phi_all.at[:, block(me, depth)], l_sem.at[2]),
        pltpu.make_async_copy(omega, omega_all.at[:, block(me, depth)], l_sem.at[3]),
        pltpu.make_async_copy(range_old, range_v, l_sem.at[4]),
        pltpu.make_async_copy(core_old, core_out, l_sem.at[5])]

    for copy in local[:2]:
        copy.start()
    for t in range(m):
        for copy in weights(chunk(t)):
            copy.start()

    barrier = pltpu.get_barrier_semaphore()
    for e in range(1, n):
        pl.semaphore_signal(barrier, inc=1, device_id={"row": peer(e)}, device_id_type=MESH)
    for d in range(1, m):
        pl.semaphore_signal(barrier, inc=1, device_id={"col": lax.rem(c + d, m)}, device_id_type=MESH)
    pl.semaphore_wait(barrier, n - 1 + m - 1)

    def window_copy(e, h):
        return remote(window.at[pl.ds(h * half, half), block(peer(e), width)], relaid.at[at(me, h), :],
                      a_s.at[e, h], a_r.at[e, h], {"row": peer(e)})

    def phi_copy(e):
        return remote(phi.at[block(peer(e), core_rows), :], phi_all.at[:, block(me, depth)],
                      p_s.at[e], p_r.at[e], {"row": peer(e)})

    for o, h in pieces:
        for e in (2 * o, 2 * o + 1):
            if e:
                window_copy(e, h).start()

    def spread_omega(o):
        return remote(omega, omega_all.at[:, block(me, depth)], g_s.at[o, 2], g_r.at[o, 2], {"row": peer(2 * o)})

    def pass_omega(o):
        place = omega_all.at[:, block(peer(2 * o), depth)]
        return remote(place, place, f_s.at[o, 2], f_r.at[o, 2], {"row": peer(1)})

    def spread_rows(o, h):
        place = gathered.at[at(me, h), :]
        return remote(place, place, g_s.at[o, h], g_r.at[o, h], {"row": peer(2 * o)})

    def pass_rows(o, h):
        place = gathered.at[at(peer(2 * o), h), :]
        return remote(place, place, f_s.at[o, h], f_r.at[o, h], {"row": peer(1)})

    for copy in local[2:]:
        copy.start()
    for e in range(1, n):
        phi_copy(e).start()
    for o in range(1, chips):
        spread_omega(o).start()
    local[3].wait()
    pass_omega(0).start()

    def swap_copy(i, d):
        return remote(xs.at[i % slots, d], xr.at[i, d], x_s.at[i, d], x_r.at[i, d], {"row": peer(1)})

    def near_copy(i, d):
        return remote(zs.at[i, d], z1r.at[i, d], z_s.at[i, d], z1_s.at[i, d], {"col": near})

    def far_copy(i, d):
        return remote(zs.at[i, d], z2r.at[i, pair], z_s.at[i, d], z2_s.at[i, pair], {"col": d})

    def back_copy(i):
        o, h = pieces[i]
        return remote(ys.at[i], yr.at[o, h], y_s.at[i], y_r.at[o, h], {"row": peer(2 * o)})

    def multiply(i):
        o, h = pieces[i]
        slot = i % slots
        if o == 0:
            local[h].wait()
        else:
            window_copy(2 * o, h).wait_recv()
        window_copy(2 * o + 1, h).wait_recv()

        @pl.loop(0, m)
        def _(t):
            d = chunk(t)
            if i == 0:
                for copy in weights(d):
                    copy.wait()
            if i >= slots:
                swap_copy(i - slots, d).wait_send()
            lhs = jnp.concatenate([relaid[at(peer(2 * o + 1), h), :], relaid[at(peer(2 * o), h), :]], axis=0)
            for weight, w, start in ((psi_v, lz, 0), (ups_v, sz, lz)):
                product = jnp.dot(lhs, weight[:, block(d, w)], preferred_element_type=F32)
                xs[slot, d, :, start:start + w] = product[:half]
                keep[slot, d, :, start:start + w] = product[half:]
            swap_copy(i, d).start()

    def combine(i):
        slot = i % slots

        @pl.loop(0, m)
        def _(t):
            d = chunk(t)
            swap_copy(i, d).wait_recv()
            total = keep[slot, d] + xr[i, d]

            @pl.when(t < first)
            def _():
                zs[i, d] = encode(total)
                near_copy(i, d).start()

            @pl.when(t >= first)
            def _():
                keep[slot, d] = total

    def relay(i):
        slot = i % slots

        @pl.loop(first, m - 1)
        def _(t):
            d = chunk(t)
            near_copy(i, d).wait_recv()
            zs[i, d] = encode(keep[slot, d] + decode(z1r[i, d]))
            far_copy(i, d).start()

    def give_back(i):
        o, h = pieces[i]
        near_copy(i, c).wait_recv()
        own_slot = own.at[h] if o == 0 else keep.at[i % slots, c]
        own_slot[...] = keep[i % slots, c] + decode(z1r[i, c])
        for g in range(m // 2):
            @pl.when(g != pair)
            def _():
                remote(zs.at[i, c], z2r.at[i, g], z_s.at[i, c], z2_s.at[i, g], {"col": near}).wait_recv()
                own_slot[...] += decode(z2r[i, g])
        if o:
            ys[i] = encode(own_slot[...])
            back_copy(i).start()

    def finish(h):
        total = own[h]
        for o in range(1, chips):
            back_copy(pieces.index((o, h))).wait_recv()
            total = total + decode(yr[o, h])
        co_out[pl.ds(h * half, half), :] = total[:, :lz]
        gathered[at(me, h), :] = total[:, lz:].astype(BF16)
        for o in range(1, chips):
            spread_rows(o, h).start()
        pass_rows(0, h).start()

    count = len(pieces)
    for step in range(count + 2):
        if step < count:
            multiply(step)
            combine(step)
        if 0 <= step - 1 < count:
            relay(step - 1)
        if 0 <= step - 2:
            give_back(step - 2)

    for h in range(2):
        finish(h)

    for o in range(1, chips):
        spread_omega(o).wait_recv()
        pass_omega(o).start()
    for h in range(2):
        for o in range(1, chips):
            spread_rows(o, h).wait_recv()
            pass_rows(o, h).start()
    for o in range(chips):
        pass_omega(o).wait_recv()
    local[4].wait()
    tile = range_tile(width)

    def range_copy(j):
        return pltpu.make_async_copy(range_v.at[:, block(j, tile)], range_out.at[:, block(j, tile)], r_sem.at[j])

    @pl.loop(0, width // tile)
    def _(j):
        range_v[:, block(j, tile)] += jnp.dot(omega_all[...], relaid[:, block(j, tile)], preferred_element_type=F32)
        range_copy(j).start()

    local[2].wait()
    local[5].wait()
    for e in range(1, n):
        phi_copy(e).wait_recv()
    for h in range(2):
        for o in range(chips):
            pass_rows(o, h).wait_recv()
    core_out[...] += jnp.dot(phi_all[...], gathered[...], preferred_element_type=F32)

    for e in range(1, n):
        phi_copy(e).wait_send()
        for h in range(2):
            window_copy(e, h).wait_send()
    for o in range(chips):
        pass_omega(o).wait_send()
        if o:
            spread_omega(o).wait_send()
        for h in range(2):
            pass_rows(o, h).wait_send()
            if o:
                spread_rows(o, h).wait_send()
    for i in range(count):
        if pieces[i][0]:
            back_copy(i).wait_send()

        @pl.loop(0, m)
        def _(d):
            if i + slots >= count:
                swap_copy(i, d).wait_send()

            @pl.when(d != c)
            def _():
                near_copy(i, d).wait_send()

    @pl.loop(0, width // tile)
    def _(j):
        range_copy(j).wait()


def range_tile(width):
    return min(width, 256)


def shards(n, m, window_rows, omega_cols, psi_rows, upsilon_rows, phi_cols, range_old, core_old):
    any_space = pl.BlockSpec(memory_space=pl.ANY)
    vmem = pl.BlockSpec(memory_space=pltpu.VMEM)
    dma = pltpu.SemaphoreType.DMA
    rows, wide = window_rows.shape
    width = wide // n
    k = omega_cols.shape[0]
    l, s = psi_rows.shape[1], upsilon_rows.shape[1]
    core_rows = phi_cols.shape[0] // n
    half, chips, cz = rows // 2, n // 2, (l + s) // m
    count = 2 * chips
    slots = min(count, 4)
    scratch = [
        pltpu.VMEM((rows * n, width), BF16), pltpu.VMEM((width, l), BF16), pltpu.VMEM((width, s), BF16),
        pltpu.VMEM((slots, m, half, cz), F32), pltpu.VMEM((count, m, half, cz), F32), pltpu.VMEM((slots, m, half, cz), F32),
        pltpu.VMEM((count, m, half, cz), BF16), pltpu.VMEM((count, m, half, cz), BF16), pltpu.VMEM((count, m // 2, half, cz), BF16),
        pltpu.VMEM((2, half, cz), F32), pltpu.VMEM((count, half, cz), BF16), pltpu.VMEM((chips, 2, half, cz), BF16),
        pltpu.VMEM((rows * n, s // m), BF16), pltpu.VMEM((core_rows, rows * n), BF16), pltpu.VMEM((k, rows * n), BF16),
        pltpu.VMEM((k, width), F32),
        dma((m, 2)), dma((6,)), dma((n, 2)), dma((n, 2)), dma((n,)), dma((n,)),
        dma((count, m)), dma((count, m)), dma((count, m)), dma((count, m)), dma((count, m // 2)),
        dma((count,)), dma((chips, 2)), dma((chips, 3)), dma((chips, 3)), dma((chips, 3)), dma((chips, 3)),
        dma((width // range_tile(width),)),
    ]
    return pl.pallas_call(
        functools.partial(sketch_kernel, n, m),
        out_shape=(
            jax.ShapeDtypeStruct((k, width), F32), jax.ShapeDtypeStruct((rows, l // m), F32),
            jax.ShapeDtypeStruct((core_rows, s // m), F32)),
        in_specs=[any_space] * 7,
        out_specs=(any_space, vmem, vmem),
        scratch_shapes=scratch,
        compiler_params=pltpu.CompilerParams(collective_id=0, has_side_effects=True, vmem_limit_bytes=LIMIT),
        name="sketch",
    )(window_rows, omega_cols, psi_rows, upsilon_rows, phi_cols, range_old, core_old)


def solution(mesh):
    placed = (
        P("row", "col"),
        P(None, "row"),
        P(("col", "row"), None),
        P(("col", "row"), None),
        P(None, "row"),
        P(None, ("col", "row")),
        P("row", "col"),
    )
    return jax.shard_map(
        functools.partial(shards, mesh.shape["row"], mesh.shape["col"]),
        mesh=mesh,
        in_specs=placed,
        out_specs=(P(None, ("col", "row")), P("row", "col"), P("row", "col")),
        check_vma=False,
    )
```

time: 192 us -> 102 us (0.53)
  Pallas kernels: 145 us -> 94.2 us
  matrix products: 31.7 us -> 0 us
  between operations: 14.1 us -> 0.66 us
  local copies, waits for them, and re-layouts: 0.68 us -> 6.22 us
    pallas_call x2 -> x1, Pallas kernels: 145 us -> 94.2 us  [shards(): pl.pallas_call(functools.partial(sketch_kernel, n, m), out_shape=(jax.Sha...]
    dot_general x4 -> x0, matrix products: 31.7 us -> none  [the longest x1 11 us: shards(): core_part = jnp.dot(relaid, upsilon_rows, preferred_element_type=f32)]
    unnamed x11 -> x7, local copies, waits for them, and re-layouts: 0.68 us -> 6.22 us
  transfers between devices with their start and end apart: 1 -> 0, of which waited for: 0 -> 0; matrix products, arithmetic and copies ran while one was open for 12% -> 0% of each run, Pallas kernels for 47% -> 0%
where the time goes in v1:
time: 102 us; the launch traced here: 101 us
  Pallas kernels  94.2 us (92%)
  local copies, waits for them, and re-layouts  6.22 us (6%)
    pallas_call x1, Pallas kernels, shards(): pl.pallas_call(functools.partial(sketch_kernel, n, m), out_shape=(jax.Sha...  94.2 us
    unnamed x7, local copies, waits for them, and re-layouts  6.22 us

profile of v1, /device:TPU:11, one launch (start us, length us, event | category | flops | bytes accessed | tf_op | source)
XLA Modules:
  0.0 101.1 jit_solution(11825941015097618009)
XLA Ops:
  0.6 94.2 %sketch.1 = (f32[512,2048]{1,0:T(8,128)}, f32[128,256]{1,0:T(8,128)}, f32[256,512]{1,0:T(8,128)}) custom-call(bf16[128,16384]{1,0:T(8,128)(2,1)} %window.1, bf16[512,128]{1,0:T(8,128)(2,1)} %omega.1, bf16[2048,1024]{1,0:T(8,128)(2,1)} %psi.1, bf16[2048,2048]{1,0:T(8,128)(2,1)} %ups.1, bf16[2048,128]{1,0:T(8,128)(2,1)} %phi.1, f32[512,2048]{1,0:T(8,128)} %range_old.1, ...), custom_call_target="tpu_custom_call" | custom-call | tf_op jit(solution)/shard_map/sketch/pallas_call | solution.py:330
  94.8 0.0 copy-start.1
  94.8 0.0 copy-start
  94.8 4.8 %copy.13 = f32[512,2048]{1,0:T(8,128)} copy(f32[512,2048]{1,0:T(8,128)} %get-tuple-element.6) | data formatting | bytes 8388608
  99.6 0.0 copy-done.1
  99.6 0.7 copy.14
  100.3 0.0 copy-done
  100.3 0.8 copy.15
Async XLA Ops:
  94.8 4.8 %copy-start.1 = (f32[128,256]{1,0:T(8,128)S(1)}, f32[128,256]{1,0:T(8,128)}, u32[]{:S(2)}) copy-start(f32[128,256]{1,0:T(8,128)} %get-tuple-element.7) | copy-start | bytes 393220
  94.8 5.4 %copy-start = (f32[256,512]{1,0:T(8,128)S(1)}, f32[256,512]{1,0:T(8,128)}, u32[]{:S(2)}) copy-start(f32[256,512]{1,0:T(8,128)} %get-tuple-element.8) | copy-start | bytes 1572868

commit v2 on v1

v2 whole, which is shorter than its diff:
```python
import contextlib
import functools
import math

import jax
import jax.numpy as jnp
from jax import lax
from jax.experimental import pallas as pl
from jax.experimental.pallas import tpu as pltpu
from jax.sharding import PartitionSpec as P

MESH = pl.DeviceIdType.MESH
LIMIT = 67043328
LEAD = 3
LAG = 2
ROOM = 13000 * 1024
F32, BF16 = jnp.float32, jnp.bfloat16


def mark(name):
    return contextlib.nullcontext()


def encode(x):
    return (x * jnp.abs(x)).astype(BF16)


def decode(y):
    y = y.astype(F32)
    return y * lax.rsqrt(jnp.maximum(jnp.abs(y), 1e-37))


def flip(index, mask, count):
    total, bit = 0, 1
    while bit < count:
        own = (index // bit) % 2
        total = total + (1 - own if mask & bit else own) * bit
        bit *= 2
    return total


def piece_order(chips):
    classes = {}
    for o in range(chips):
        classes.setdefault(bin(o).count("1"), []).append(o)
    return [(o, h) for k in sorted(classes) for h in range(2) for o in classes[k]]


def sketch_kernel(n, m, window, omega, psi, ups, phi, range_old, core_old, range_v, co_out, core_out,
                  relaid, psi_v, ups_v, xs, xr, keep, zs, z1r, z2r, own, ys, yr, gathered, phi_all, omega_all,
                  w_sem, l_sem, a_s, a_r, p_s, p_r, x_s, x_r, z_s, z1_s, z2_s, y_s, y_r, g_s, g_r, f_s, f_r):
    me, c = lax.axis_index("row"), lax.axis_index("col")
    chips = n // 2
    rows, width = window.shape[0], relaid.shape[1]
    half = rows // 2
    lz = psi_v.shape[1] // m
    sz = ups_v.shape[1] // m
    cz = lz + sz
    slots = keep.shape[0]
    core_rows, depth = phi_all.shape[0], phi.shape[1]
    pieces = piece_order(chips)
    odd = c % 2
    side = c + odd * (m - 1 - 2 * c)
    first = m - 1 - side
    near = c + 1 - 2 * odd
    pair = c // 2

    def at(r, h):
        return pl.ds(pl.multiple_of(r * rows + h * half, half), half)

    def block(r, size):
        return pl.ds(pl.multiple_of(r * size, size), size)

    def peer(mask):
        return flip(me, mask, n)

    def chunk(t):
        ahead = jnp.where(t < first, m - 1 - t, jnp.where(t < m - 1, t - first, side))
        return ahead + odd * (m - 1 - 2 * ahead)

    def remote(src, dst, send_sem, recv_sem, device):
        return pltpu.make_async_remote_copy(
            src_ref=src, dst_ref=dst, send_sem=send_sem, recv_sem=recv_sem, device_id=device, device_id_type=MESH)

    def sent(ref, sem):
        remote(ref, ref, sem, y_r.at[0], {"row": peer(1)}).wait_send()

    def received(ref, sem):
        remote(ref, ref, y_s, sem, {"row": peer(1)}).wait_recv()

    def weights(d):
        return (
            pltpu.make_async_copy(psi.at[:, block(d, lz)], psi_v.at[:, block(d, lz)], w_sem.at[d, 0]),
            pltpu.make_async_copy(ups.at[:, block(d, sz)], ups_v.at[:, block(d, sz)], w_sem.at[d, 1]))

    local = [
        pltpu.make_async_copy(window.at[pl.ds(h * half, half), block(me, width)], relaid.at[at(me, h), :], l_sem.at[h])
        for h in range(2)]
    local += [
        pltpu.make_async_copy(phi.at[block(me, core_rows), :], phi_all.at[:, block(me, depth)], l_sem.at[2]),
        pltpu.make_async_copy(omega, omega_all.at[:, block(me, depth)], l_sem.at[3]),
        pltpu.make_async_copy(range_old, range_v, l_sem.at[4]),
        pltpu.make_async_copy(core_old, core_out, l_sem.at[5])]

    for copy in local[:2]:
        copy.start()
    for t in range(m):
        for copy in weights(chunk(t)):
            copy.start()

    barrier = pltpu.get_barrier_semaphore()
    for e in range(1, n):
        pl.semaphore_signal(barrier, inc=1, device_id={"row": peer(e)}, device_id_type=MESH)
    for d in range(1, m):
        pl.semaphore_signal(barrier, inc=1, device_id={"col": lax.rem(c + d, m)}, device_id_type=MESH)
    pl.semaphore_wait(barrier, n - 1 + m - 1)

    def window_copy(e, h):
        return remote(window.at[pl.ds(h * half, half), block(peer(e), width)], relaid.at[at(me, h), :],
                      a_s, a_r.at[e, h], {"row": peer(e)})

    def phi_copy(e):
        return remote(phi.at[block(peer(e), core_rows), :], phi_all.at[:, block(me, depth)],
                      p_s, p_r, {"row": peer(e)})

    def send_window(i):
        o, h = pieces[i]
        for e in (2 * o, 2 * o + 1):
            if e:
                window_copy(e, h).start()

    def distant(i):
        return bin(pieces[i][0]).count("1") > 1

    for i in range(len(pieces)):
        if not distant(i):
            send_window(i)

    def spread_omega(o):
        return remote(omega, omega_all.at[:, block(me, depth)], g_s.at[1], g_r.at[2], {"row": peer(2 * o)})

    def pass_omega(o):
        place = omega_all.at[:, block(peer(2 * o), depth)]
        return remote(place, place, f_s.at[1], f_r.at[2], {"row": peer(1)})

    def spread_rows(o, h):
        place = gathered.at[at(me, h), :]
        return remote(place, place, g_s.at[0], g_r.at[h], {"row": peer(2 * o)})

    def pass_rows(o, h):
        place = gathered.at[at(peer(2 * o), h), :]
        return remote(place, place, f_s.at[0], f_r.at[h], {"row": peer(1)})

    for copy in local[2:]:
        copy.start()

    def send_small():
        for o in range(1, chips):
            spread_omega(o).start()
        local[3].wait()
        pass_omega(0).start()
        for e in range(1, n):
            phi_copy(e).start()

    def swap_copy(i, d):
        return remote(xs.at[i % slots, d], xr.at[i, d], x_s.at[i % slots], x_r.at[i % 2, d], {"row": peer(1)})

    def near_copy(i, d):
        return remote(zs.at[i, d], z1r.at[i, d], z_s, z1_s.at[i, d], {"col": near})

    def far_copy(i, d):
        return remote(zs.at[i, d], z2r.at[i, pair], z_s, z2_s.at[i, pair], {"col": d})

    def back_copy(i):
        o, h = pieces[i]
        return remote(ys.at[i], yr.at[h, o], y_s, y_r.at[h], {"row": peer(2 * o)})

    def multiply(i):
        o, h = pieces[i]
        slot = i % slots
        if o == 0:
            local[h].wait()
        else:
            window_copy(2 * o, h).wait_recv()
        window_copy(2 * o + 1, h).wait_recv()
        if i >= slots:
            sent(xs.at[slot], x_s.at[slot])

        def product(t):
            d = chunk(t)
            if i == 0:
                for copy in weights(d):
                    copy.wait()
            lhs = jnp.concatenate([relaid[at(peer(2 * o + 1), h), :], relaid[at(peer(2 * o), h), :]], axis=0)
            for weight, w, start in ((psi_v, lz, 0), (ups_v, sz, lz)):
                both = jnp.dot(lhs, weight[:, block(d, w)], preferred_element_type=F32)
                xs[slot, d, :, start:start + w] = both[:half]
                keep[slot, d, :, start:start + w] = both[half:]
            swap_copy(i, d).start()

        def combine(t):
            d = chunk(t)
            swap_copy(i, d).wait_recv()
            total = keep[slot, d] + xr[i, d]

            @pl.when(t < first)
            def _():
                zs[i, d] = encode(total)
                near_copy(i, d).start()

            @pl.when(t >= first)
            def _():
                keep[slot, d] = total

        @pl.loop(0, m + LAG)
        def _(t):
            @pl.when(t < m)
            def _():
                product(t)

            @pl.when(t >= LAG)
            def _():
                combine(t - LAG)

    def relay(i):
        slot = i % slots

        @pl.loop(first, m - 1)
        def _(t):
            d = chunk(t)
            near_copy(i, d).wait_recv()
            zs[i, d] = encode(keep[slot, d] + decode(z1r[i, d]))
            far_copy(i, d).start()

    def give_back(i):
        o, h = pieces[i]
        near_copy(i, c).wait_recv()
        own_slot = own.at[h] if o == 0 else keep.at[i % slots, c]
        own_slot[...] = keep[i % slots, c] + decode(z1r[i, c])
        for g in range(m // 2):
            @pl.when(g != pair)
            def _():
                remote(zs.at[i, c], z2r.at[i, g], z_s, z2_s.at[i, g], {"col": near}).wait_recv()
                own_slot[...] += decode(z2r[i, g])
        if o:
            ys[i] = encode(own_slot[...])
            back_copy(i).start()

    def finish(h):
        received(yr.at[h, 1:], y_r.at[h])
        total = own[h]
        for o in range(1, chips):
            total = total + decode(yr[h, o])
        co_out[pl.ds(h * half, half), :] = total[:, :lz]
        gathered[at(me, h), :] = total[:, lz:].astype(BF16)
        for o in range(1, chips):
            spread_rows(o, h).start()
        pass_rows(0, h).start()

    tile = range_tile(width)
    tiles = width // tile

    def forward_omega():
        received(omega_all.at[:, pl.ds(0, (chips - 1) * depth)], g_r.at[2])
        for o in range(1, chips):
            pass_omega(o).start()

    def update_range():
        local[4].wait()
        received(omega_all.at[:, pl.ds(0, chips * depth)], f_r.at[2])

        @pl.loop(0, tiles)
        def _(j):
            range_v[:, block(j, tile)] += jnp.dot(omega_all[...], relaid[:, block(j, tile)], preferred_element_type=F32)

    def forward_rows(h):
        received(gathered.at[pl.ds(0, (chips - 1) * half), :], g_r.at[h])
        for o in range(1, chips):
            pass_rows(o, h).start()

    def wait_all():
        local[2].wait()
        local[5].wait()
        received(phi_all.at[:, pl.ds(0, (n - 1) * depth)], p_r)
        for h in range(2):
            received(gathered.at[pl.ds(0, chips * half), :], f_r.at[h])

    def update_core():
        core_out[...] += jnp.dot(phi_all[...], gathered[...], preferred_element_type=F32)

    count = len(pieces)

    def drain():
        sent(window.at[:, pl.ds(0, (n - 1) * width)], a_s)
        for i in range(count - slots, count):
            sent(xs.at[i % slots], x_s.at[i % slots])

    def drain_all():
        sent(zs.at[:, pl.ds(0, m - 1)], z_s)
        sent(ys.at[pl.ds(0, count - 2)], y_s)
        sent(phi.at[pl.ds(0, (n - 1) * core_rows), :], p_s)
        sent(omega_all.at[:, pl.ds(0, (chips - 1) * depth)], g_s.at[1])
        sent(omega_all.at[:, pl.ds(0, chips * depth)], f_s.at[1])
        sent(gathered.at[pl.ds(0, (chips - 1) * rows), :], g_s.at[0])
        sent(gathered.at[pl.ds(0, chips * rows), :], f_s.at[0])

    plan = []
    for step in range(count):
        plan += [(send_window, i) for i in range(count) if distant(i) and step == max(i - LEAD, 0)]
        if step == count - 2:
            plan.append((send_small,))
        plan.append((multiply, step))
        if step and step < count - 1:
            plan.append((relay, step - 1))
        if step >= 2:
            plan.append((give_back, step - 2))
        if step == count - 2:
            plan.append((relay, step))
    plan += [
        (give_back, count - 2), (relay, count - 1), (forward_omega,), (give_back, count - 1),
        (finish, 0), (finish, 1), (drain,), (update_range,), (forward_rows, 0), (forward_rows, 1), (wait_all,),
        (update_core,), (drain_all,)]
    for act, *which in plan:
        with mark("_".join([act.__name__, *map(str, which[:1])])):
            act(*which)


def store_kernel(*refs):
    *refs, sem = refs
    count = len(refs) // 2
    copies = [pltpu.make_async_copy(refs[i], refs[count + i], sem.at[i]) for i in range(count)]
    for copy in copies:
        copy.start()
    for copy in copies:
        copy.wait()


def range_tile(width):
    return min(width, 256)


def shards(n, m, window_rows, omega_cols, psi_rows, upsilon_rows, phi_cols, range_old, core_old):
    any_space = pl.BlockSpec(memory_space=pl.ANY)
    vmem = pl.BlockSpec(memory_space=pltpu.VMEM)
    dma = pltpu.SemaphoreType.DMA
    rows, wide = window_rows.shape
    width = wide // n
    k = omega_cols.shape[0]
    l, s = psi_rows.shape[1], upsilon_rows.shape[1]
    core_rows = phi_cols.shape[0] // n
    half, chips, cz = rows // 2, n // 2, (l + s) // m
    count = 2 * chips
    slots = min(count, 4)
    scratch = [
        pltpu.VMEM((rows * n, width), BF16), pltpu.VMEM((width, l), BF16), pltpu.VMEM((width, s), BF16),
        pltpu.VMEM((slots, m, half, cz), F32), pltpu.VMEM((count, m, half, cz), F32), pltpu.VMEM((slots, m, half, cz), F32),
        pltpu.VMEM((count, m, half, cz), BF16), pltpu.VMEM((count, m, half, cz), BF16), pltpu.VMEM((count, m // 2, half, cz), BF16),
        pltpu.VMEM((2, half, cz), F32), pltpu.VMEM((count, half, cz), BF16), pltpu.VMEM((2, chips, half, cz), BF16),
        pltpu.VMEM((rows * n, s // m), BF16), pltpu.VMEM((core_rows, rows * n), BF16), pltpu.VMEM((k, rows * n), BF16),
        dma((m, 2)), dma((6,)), dma, dma((n, 2)), dma, dma,
        dma((slots,)), dma((2, m)), dma, dma((count, m)), dma((count, m // 2)),
        dma, dma((2,)), dma((2,)), dma((3,)), dma((2,)), dma((3,)),
    ]
    outputs = (
        jax.ShapeDtypeStruct((k, width), F32), jax.ShapeDtypeStruct((rows, l // m), F32),
        jax.ShapeDtypeStruct((core_rows, s // m), F32))
    output_bytes = sum(4 * math.prod(out.shape) for out in outputs)
    results = pl.pallas_call(
        functools.partial(sketch_kernel, n, m),
        out_shape=outputs,
        in_specs=[any_space] * 7,
        out_specs=(vmem, vmem, vmem),
        scratch_shapes=scratch,
        compiler_params=pltpu.CompilerParams(collective_id=0, has_side_effects=True, vmem_limit_bytes=LIMIT - output_bytes - ROOM),
        name="sketch",
    )(*(pltpu.with_memory_space_constraint(x, pltpu.HBM) for x in (
        window_rows, omega_cols, psi_rows, upsilon_rows, phi_cols, range_old, core_old)))
    return pl.pallas_call(
        store_kernel,
        out_shape=outputs,
        in_specs=[vmem] * 3,
        out_specs=[any_space] * 3,
        scratch_shapes=[dma((3,))],
        compiler_params=pltpu.CompilerParams(vmem_limit_bytes=1024 * 1024),
        name="store",
    )(*results)


def solution(mesh):
    placed = (
        P("row", "col"),
        P(None, "row"),
        P(("col", "row"), None),
        P(("col", "row"), None),
        P(None, "row"),
        P(None, ("col", "row")),
        P("row", "col"),
    )
    return jax.shard_map(
        functools.partial(shards, mesh.shape["row"], mesh.shape["col"]),
        mesh=mesh,
        in_specs=placed,
        out_specs=(P(None, ("col", "row")), P("row", "col"), P("row", "col")),
        check_vma=False,
    )
```

time: 102 us -> 84 us (0.82)
  the two profiles are of different devices: /device:TPU:11 before, /device:TPU:1 now
where the time goes in v2:
time: 84 us; the launch traced here: 83.8 us
  Pallas kernels  83.2 us (99%)
    pallas_call x1, Pallas kernels, shards(): pl.pallas_call(functools.partial(sketch_kernel, n, m), out_shape=outputs,...  80.9 us
    pallas_call x1, Pallas kernels, shards(): pl.pallas_call(store_kernel, out_shape=outputs, in_specs=[vmem] * 3, out_...  2.24 us

profile of v2, /device:TPU:1, one launch (start us, length us, event | category | flops | bytes accessed | tf_op | source)
XLA Modules:
  0.0 83.8 jit_solution(10023977601951043892)
XLA Ops:
  0.6 80.9 %sketch.1 = (f32[512,2048]{1,0:T(8,128)S(1)}, f32[128,256]{1,0:T(8,128)S(1)}, f32[256,512]{1,0:T(8,128)S(1)}) custom-call(bf16[128,16384]{1,0:T(8,128)(2,1)} %window.1, bf16[512,128]{1,0:T(8,128)(2,1)} %omega.1, bf16[2048,1024]{1,0:T(8,128)(2,1)} %psi.1, bf16[2048,2048]{1,0:T(8,128)(2,1)} %ups.1, bf16[2048,128]{1,0:T(8,128)(2,1)} %phi.1, ...), custom_call_target="tpu_custom_call" | custom-call | tf_op jit(solution)/shard_map/sketch/pallas_call | solution.py:368
  81.6 2.2 %store.1 = (f32[512,2048]{1,0:T(8,128)}, f32[128,256]{1,0:T(8,128)}, f32[256,512]{1,0:T(8,128)}) custom-call(f32[512,2048]{1,0:T(8,128)S(1)} %get-tuple-element.6.refs_0_, f32[128,256]{1,0:T(8,128)S(1)} %get-tuple-element.7.refs_1_, f32[256,512]{1,0:T(8,128)S(1)} %get-tuple-element.8.refs_2_), custom_call_target="tpu_custom_call" | custom-call | tf_op jit(solution)/shard_map/store/pallas_call | solution.py:378

commit v3 on v2

--- a/solution.py
+++ b/solution.py
@@ -58,6 +58,7 @@
     cz = lz + sz
     slots = keep.shape[0]
     core_rows, depth = phi_all.shape[0], phi.shape[1]
+    dims = chips.bit_length() - 1
     pieces = piece_order(chips)
     odd = c % 2
     side = c + odd * (m - 1 - 2 * c)
@@ -90,8 +91,8 @@
 
     def weights(d):
         return (
-            pltpu.make_async_copy(psi.at[:, block(d, lz)], psi_v.at[:, block(d, lz)], w_sem.at[d, 0]),
-            pltpu.make_async_copy(ups.at[:, block(d, sz)], ups_v.at[:, block(d, sz)], w_sem.at[d, 1]))
+            pltpu.make_async_copy(psi.at[:, block(d, lz)], psi_v.at[:, block(d, lz)], w_sem.at[d]),
+            pltpu.make_async_copy(ups.at[:, block(d, sz)], ups_v.at[:, block(d, sz)], w_sem.at[d]))
 
     local = [
         pltpu.make_async_copy(window.at[pl.ds(h * half, half), block(me, width)], relaid.at[at(me, h), :], l_sem.at[h])
@@ -102,22 +103,29 @@
         pltpu.make_async_copy(range_old, range_v, l_sem.at[4]),
         pltpu.make_async_copy(core_old, core_out, l_sem.at[5])]
 
+    def linked(d):
+        low, high = jnp.minimum(c, d), jnp.maximum(c, d)
+        return (d != c) & ((low // 2 == high // 2) | (high % 2 == 0) | (low % 2 == 1))
+
+    barrier = pltpu.get_barrier_semaphore()
+    greeted = n - 1
+    for d in range(m):
+        @pl.when(linked(d))
+        def _():
+            pl.semaphore_signal(barrier, inc=1, device_id={"col": d}, device_id_type=MESH)
+        greeted = greeted + jnp.where(linked(d), 1, 0)
+    for e in reversed(range(1, n)):
+        pl.semaphore_signal(barrier, inc=1, device_id={"row": peer(e)}, device_id_type=MESH)
     for copy in local[:2]:
         copy.start()
     for t in range(m):
         for copy in weights(chunk(t)):
             copy.start()
-
-    barrier = pltpu.get_barrier_semaphore()
-    for e in range(1, n):
-        pl.semaphore_signal(barrier, inc=1, device_id={"row": peer(e)}, device_id_type=MESH)
-    for d in range(1, m):
-        pl.semaphore_signal(barrier, inc=1, device_id={"col": lax.rem(c + d, m)}, device_id_type=MESH)
-    pl.semaphore_wait(barrier, n - 1 + m - 1)
+    pl.semaphore_wait(barrier, greeted)
 
     def window_copy(e, h):
         return remote(window.at[pl.ds(h * half, half), block(peer(e), width)], relaid.at[at(me, h), :],
-                      a_s, a_r.at[e, h], {"row": peer(e)})
+                      a_s, a_r.at[e // 2, h], {"row": peer(e)})
 
     def phi_copy(e):
         return remote(phi.at[block(peer(e), core_rows), :], phi_all.at[:, block(me, depth)],
@@ -129,15 +137,29 @@
             if e:
                 window_copy(e, h).start()
 
+    def distant_chip(o):
+        return bin(o).count("1") > 1
+
     def distant(i):
-        return bin(pieces[i][0]).count("1") > 1
+        return distant_chip(pieces[i][0])
 
     for i in range(len(pieces)):
         if not distant(i):
             send_window(i)
 
-    def spread_omega(o):
-        return remote(omega, omega_all.at[:, block(me, depth)], g_s.at[1], g_r.at[2], {"row": peer(2 * o)})
+    def omega_copy(o, g, j):
+        rows_g = pl.ds(g * (omega.shape[0] // 2), omega.shape[0] // 2)
+        place = omega_all.at[rows_g, block(peer(2 * o), depth)]
+        source = place if o else omega.at[rows_g, :]
+        return remote(source, place, g_s.at[1], g_r.at[2 + j], {"row": peer(2 << (j + g) % dims)})
+
+    def omega_step(j):
+        if j:
+            received(omega_all.at[:, pl.ds(0, depth << (j - 1))], g_r.at[1 + j])
+        for o in range(chips):
+            for g in range(2):
+                if all((o & 1 << (i + g) % dims) == 0 for i in range(j, dims)):
+                    omega_copy(o, g, j).start()
 
     def pass_omega(o):
         place = omega_all.at[:, block(peer(2 * o), depth)]
@@ -155,12 +177,14 @@
         copy.start()
 
     def send_small():
-        for o in range(1, chips):
-            spread_omega(o).start()
+        omega_step(0)
         local[3].wait()
         pass_omega(0).start()
+
+    def send_phi(part):
         for e in range(1, n):
-            phi_copy(e).start()
+            if (2 if distant_chip(e // 2) else e % 2) == part:
+                phi_copy(e).start()
 
     def swap_copy(i, d):
         return remote(xs.at[i % slots, d], xr.at[i, d], x_s.at[i % slots], x_r.at[i % 2, d], {"row": peer(1)})
@@ -169,28 +193,27 @@
         return remote(zs.at[i, d], z1r.at[i, d], z_s, z1_s.at[i, d], {"col": near})
 
     def far_copy(i, d):
-        return remote(zs.at[i, d], z2r.at[i, pair], z_s, z2_s.at[i, pair], {"col": d})
-
-    def back_copy(i):
-        o, h = pieces[i]
-        return remote(ys.at[i], yr.at[h, o], y_s, y_r.at[h], {"row": peer(2 * o)})
+        return remote(zs.at[i, d], z2r.at[i, pair], z_s, z2_s.at[i], {"col": d})
+
+    def back_copy(o, h):
+        return remote(ys.at[h, o], yr.at[h, o], y_s, y_r.at[h], {"row": peer(2 * o)})
 
     def multiply(i):
         o, h = pieces[i]
         slot = i % slots
         if o == 0:
             local[h].wait()
+            window_copy(1, h).wait_recv()
         else:
-            window_copy(2 * o, h).wait_recv()
-        window_copy(2 * o + 1, h).wait_recv()
+            received(relaid.at[pl.ds(0, 2 * half), :], a_r.at[o, h])
         if i >= slots:
             sent(xs.at[slot], x_s.at[slot])
 
         def product(t):
             d = chunk(t)
             if i == 0:
-                for copy in weights(d):
-                    copy.wait()
+                both = ups_v.at[:, pl.ds(0, cz)]
+                pltpu.make_async_copy(both, both, w_sem.at[d]).wait()
             lhs = jnp.concatenate([relaid[at(peer(2 * o + 1), h), :], relaid[at(peer(2 * o), h), :]], axis=0)
             for weight, w, start in ((psi_v, lz, 0), (ups_v, sz, lz)):
                 both = jnp.dot(lhs, weight[:, block(d, w)], preferred_element_type=F32)
@@ -235,20 +258,21 @@
     def give_back(i):
         o, h = pieces[i]
         near_copy(i, c).wait_recv()
-        own_slot = own.at[h] if o == 0 else keep.at[i % slots, c]
-        own_slot[...] = keep[i % slots, c] + decode(z1r[i, c])
+        total = own.at[h, o]
+        total[...] = keep[i % slots, c] + decode(z1r[i, c])
+        if m > 2:
+            received(z2r.at[i, pl.ds(0, m // 2 - 1)], z2_s.at[i])
         for g in range(m // 2):
             @pl.when(g != pair)
             def _():
-                remote(zs.at[i, c], z2r.at[i, g], z_s, z2_s.at[i, g], {"col": near}).wait_recv()
-                own_slot[...] += decode(z2r[i, g])
+                total[...] += decode(z2r[i, g])
         if o:
-            ys[i] = encode(own_slot[...])
-            back_copy(i).start()
+            ys[h, o] = encode(total[...])
+            back_copy(o, h).start()
 
     def finish(h):
-        received(yr.at[h, 1:], y_r.at[h])
-        total = own[h]
+        received(yr.at[h, pl.ds(1, chips - 1)], y_r.at[h])
+        total = own[h, 0]
         for o in range(1, chips):
             total = total + decode(yr[h, o])
         co_out[pl.ds(h * half, half), :] = total[:, :lz]
@@ -261,7 +285,7 @@
     tiles = width // tile
 
     def forward_omega():
-        received(omega_all.at[:, pl.ds(0, (chips - 1) * depth)], g_r.at[2])
+        received(omega_all.at[:, pl.ds(0, depth << (dims - 1))], g_r.at[1 + dims])
         for o in range(1, chips):
             pass_omega(o).start()
 
@@ -297,7 +321,7 @@
 
     def drain_all():
         sent(zs.at[:, pl.ds(0, m - 1)], z_s)
-        sent(ys.at[pl.ds(0, count - 2)], y_s)
+        sent(ys.at[:, pl.ds(1, chips - 1)], y_s)
         sent(phi.at[pl.ds(0, (n - 1) * core_rows), :], p_s)
         sent(omega_all.at[:, pl.ds(0, (chips - 1) * depth)], g_s.at[1])
         sent(omega_all.at[:, pl.ds(0, chips * depth)], f_s.at[1])
@@ -309,6 +333,7 @@
         plan += [(send_window, i) for i in range(count) if distant(i) and step == max(i - LEAD, 0)]
         if step == count - 2:
             plan.append((send_small,))
+            plan += [(send_phi, p) for p in range(3)]
         plan.append((multiply, step))
         if step and step < count - 1:
             plan.append((relay, step - 1))
@@ -316,10 +341,11 @@
             plan.append((give_back, step - 2))
         if step == count - 2:
             plan.append((relay, step))
+    plan += [(give_back, count - 2)]
+    plan += [(omega_step, j) for j in range(1, dims)]
     plan += [
-        (give_back, count - 2), (relay, count - 1), (forward_omega,), (give_back, count - 1),
-        (finish, 0), (finish, 1), (drain,), (update_range,), (forward_rows, 0), (forward_rows, 1), (wait_all,),
-        (update_core,), (drain_all,)]
+        (relay, count - 1), (give_back, count - 1), (forward_omega,), (finish, 0), (finish, 1), (drain,), (update_range,),
+        (forward_rows, 0), (forward_rows, 1), (wait_all,), (update_core,), (drain_all,)]
     for act, *which in plan:
         with mark("_".join([act.__name__, *map(str, which[:1])])):
             act(*which)
@@ -355,11 +381,11 @@
         pltpu.VMEM((rows * n, width), BF16), pltpu.VMEM((width, l), BF16), pltpu.VMEM((width, s), BF16),
         pltpu.VMEM((slots, m, half, cz), F32), pltpu.VMEM((count, m, half, cz), F32), pltpu.VMEM((slots, m, half, cz), F32),
         pltpu.VMEM((count, m, half, cz), BF16), pltpu.VMEM((count, m, half, cz), BF16), pltpu.VMEM((count, m // 2, half, cz), BF16),
-        pltpu.VMEM((2, half, cz), F32), pltpu.VMEM((count, half, cz), BF16), pltpu.VMEM((2, chips, half, cz), BF16),
+        pltpu.VMEM((2, chips, half, cz), F32), pltpu.VMEM((2, chips, half, cz), BF16), pltpu.VMEM((2, chips, half, cz), BF16),
         pltpu.VMEM((rows * n, s // m), BF16), pltpu.VMEM((core_rows, rows * n), BF16), pltpu.VMEM((k, rows * n), BF16),
-        dma((m, 2)), dma((6,)), dma, dma((n, 2)), dma, dma,
-        dma((slots,)), dma((2, m)), dma, dma((count, m)), dma((count, m // 2)),
-        dma, dma((2,)), dma((2,)), dma((3,)), dma((2,)), dma((3,)),
+        dma((m,)), dma((6,)), dma, dma((chips, 2)), dma, dma,
+        dma((slots,)), dma((2, m)), dma, dma((count, m)), dma((count,)),
+        dma, dma((2,)), dma((2,)), dma((2 + chips.bit_length() - 1,)), dma((2,)), dma((3,)),
     ]
     outputs = (
         jax.ShapeDtypeStruct((k, width), F32), jax.ShapeDtypeStruct((rows, l // m), F32),

time: 84 us -> 81.5 us (0.970)
  the two profiles are of different devices: /device:TPU:1 before, /device:TPU:11 now
where the time goes in v3:
time: 81.5 us; the launch traced here: 80.5 us
  Pallas kernels  79.9 us (98%)
    pallas_call x1, Pallas kernels, shards(): pl.pallas_call(functools.partial(sketch_kernel, n, m), out_shape=outputs,...  77.6 us
    pallas_call x1, Pallas kernels, shards(): pl.pallas_call(store_kernel, out_shape=outputs, in_specs=[vmem] * 3, out_...  2.24 us

profile of v3, /device:TPU:11, one launch (start us, length us, event | category | flops | bytes accessed | tf_op | source)
XLA Modules:
  0.0 80.5 jit_solution(3559853763862748694)
XLA Ops:
  0.6 77.6 %sketch.1 = (f32[512,2048]{1,0:T(8,128)S(1)}, f32[128,256]{1,0:T(8,128)S(1)}, f32[256,512]{1,0:T(8,128)S(1)}) custom-call(bf16[128,16384]{1,0:T(8,128)(2,1)} %window.1, bf16[512,128]{1,0:T(8,128)(2,1)} %omega.1, bf16[2048,1024]{1,0:T(8,128)(2,1)} %psi.1, bf16[2048,2048]{1,0:T(8,128)(2,1)} %ups.1, bf16[2048,128]{1,0:T(8,128)(2,1)} %phi.1, ...), custom_call_target="tpu_custom_call" | custom-call | tf_op jit(solution)/shard_map/sketch/pallas_call | solution.py:394
  78.3 2.2 %store.1 = (f32[512,2048]{1,0:T(8,128)}, f32[128,256]{1,0:T(8,128)}, f32[256,512]{1,0:T(8,128)}) custom-call(f32[512,2048]{1,0:T(8,128)S(1)} %get-tuple-element.6.refs_0_, f32[128,256]{1,0:T(8,128)S(1)} %get-tuple-element.7.refs_1_, f32[256,512]{1,0:T(8,128)S(1)} %get-tuple-element.8.refs_2_), custom_call_target="tpu_custom_call" | custom-call | tf_op jit(solution)/shard_map/store/pallas_call | solution.py:404

commit v4 on v3

--- a/solution.py
+++ b/solution.py
@@ -48,7 +48,7 @@
 
 def sketch_kernel(n, m, window, omega, psi, ups, phi, range_old, core_old, range_v, co_out, core_out,
                   relaid, psi_v, ups_v, xs, xr, keep, zs, z1r, z2r, own, ys, yr, gathered, phi_all, omega_all,
-                  w_sem, l_sem, a_s, a_r, p_s, p_r, x_s, x_r, z_s, z1_s, z2_s, y_s, y_r, g_s, g_r, f_s, f_r):
+                  w_sem, l_sem, a_s, a_r, p_s, p_r, x_s, x_r, z_s, z1_s, z2_s, y_s, y_r, g_s, g_r, f_s, f_r, q_s, q_r):
     me, c = lax.axis_index("row"), lax.axis_index("col")
     chips = n // 2
     rows, width = window.shape[0], relaid.shape[1]
@@ -89,6 +89,11 @@
     def received(ref, sem):
         remote(ref, ref, y_s, sem, {"row": peer(1)}).wait_recv()
 
+    share = core_rows // m
+
+    def phi_rows(r):
+        return pl.ds(pl.multiple_of(r * core_rows + c * share, share), share)
+
     def weights(d):
         return (
             pltpu.make_async_copy(psi.at[:, block(d, lz)], psi_v.at[:, block(d, lz)], w_sem.at[d]),
@@ -98,7 +103,7 @@
         pltpu.make_async_copy(window.at[pl.ds(h * half, half), block(me, width)], relaid.at[at(me, h), :], l_sem.at[h])
         for h in range(2)]
     local += [
-        pltpu.make_async_copy(phi.at[block(me, core_rows), :], phi_all.at[:, block(me, depth)], l_sem.at[2]),
+        pltpu.make_async_copy(phi.at[phi_rows(me), :], phi_all.at[block(c, share), block(me, depth)], l_sem.at[2]),
         pltpu.make_async_copy(omega, omega_all.at[:, block(me, depth)], l_sem.at[3]),
         pltpu.make_async_copy(range_old, range_v, l_sem.at[4]),
         pltpu.make_async_copy(core_old, core_out, l_sem.at[5])]
@@ -128,8 +133,36 @@
                       a_s, a_r.at[e // 2, h], {"row": peer(e)})
 
     def phi_copy(e):
-        return remote(phi.at[block(peer(e), core_rows), :], phi_all.at[:, block(me, depth)],
-                      p_s, p_r, {"row": peer(e)})
+        return remote(phi.at[phi_rows(peer(e)), :], phi_all.at[block(c, share), block(me, depth)], p_s, p_r, {"row": peer(e)})
+
+    def ring_copy(way, step):
+        quarter = phi_all.at[block(c - way * (step - 1), share), :]
+        return remote(quarter, quarter, q_s.at[(way + 1) // 2, step - 1], q_r.at[(way + 1) // 2, step - 1], {"col": c + way})
+
+    def ring_sends(way, step):
+        source, target = c - way * (step - 1), c + way
+        return (source >= 0) & (source < m) & (target >= 0) & (target < m)
+
+    def ring_gets(way, step):
+        source = c - way * step
+        return (source >= 0) & (source < m)
+
+    def ring_wait(step):
+        for way in (-1, 1):
+            @pl.when(ring_gets(way, step))
+            def _():
+                received(phi_all.at[pl.ds(0, share), :], q_r.at[(way + 1) // 2, step - 1])
+
+    def ring_phi(step):
+        if step == 1:
+            local[2].wait()
+            received(phi_all.at[pl.ds(0, share), pl.ds(0, (n - 1) * depth)], p_r)
+        else:
+            ring_wait(step - 1)
+        for way in (-1, 1):
+            @pl.when(ring_sends(way, step))
+            def _():
+                ring_copy(way, step).start()
 
     def send_window(i):
         o, h = pieces[i]
@@ -181,10 +214,9 @@
         local[3].wait()
         pass_omega(0).start()
 
-    def send_phi(part):
+    def send_phi():
         for e in range(1, n):
-            if (2 if distant_chip(e // 2) else e % 2) == part:
-                phi_copy(e).start()
+            phi_copy(e).start()
 
     def swap_copy(i, d):
         return remote(xs.at[i % slots, d], xr.at[i, d], x_s.at[i % slots], x_r.at[i % 2, d], {"row": peer(1)})
@@ -303,9 +335,8 @@
             pass_rows(o, h).start()
 
     def wait_all():
-        local[2].wait()
         local[5].wait()
-        received(phi_all.at[:, pl.ds(0, (n - 1) * depth)], p_r)
+        ring_wait(m - 1)
         for h in range(2):
             received(gathered.at[pl.ds(0, chips * half), :], f_r.at[h])
 
@@ -322,7 +353,13 @@
     def drain_all():
         sent(zs.at[:, pl.ds(0, m - 1)], z_s)
         sent(ys.at[:, pl.ds(1, chips - 1)], y_s)
-        sent(phi.at[pl.ds(0, (n - 1) * core_rows), :], p_s)
+        sent(phi.at[pl.ds(0, (n - 1) * share), :], p_s)
+        for step in range(1, m):
+            for way in (-1, 1):
+                @pl.when(ring_sends(way, step))
+                def _():
+                    sent(phi_all.at[pl.ds(0, share), :], q_s.at[(way + 1) // 2, step - 1])
+
         sent(omega_all.at[:, pl.ds(0, (chips - 1) * depth)], g_s.at[1])
         sent(omega_all.at[:, pl.ds(0, chips * depth)], f_s.at[1])
         sent(gathered.at[pl.ds(0, (chips - 1) * rows), :], g_s.at[0])
@@ -332,8 +369,7 @@
     for step in range(count):
         plan += [(send_window, i) for i in range(count) if distant(i) and step == max(i - LEAD, 0)]
         if step == count - 2:
-            plan.append((send_small,))
-            plan += [(send_phi, p) for p in range(3)]
+            plan += [(send_phi,), (send_small,)]
         plan.append((multiply, step))
         if step and step < count - 1:
             plan.append((relay, step - 1))
@@ -344,7 +380,8 @@
     plan += [(give_back, count - 2)]
     plan += [(omega_step, j) for j in range(1, dims)]
     plan += [
-        (relay, count - 1), (give_back, count - 1), (forward_omega,), (finish, 0), (finish, 1), (drain,), (update_range,),
+        (relay, count - 1), (ring_phi, 1), (give_back, count - 1), (ring_phi, 2), (forward_omega,), (finish, 0), (finish, 1),
+        *((ring_phi, step) for step in range(3, m)), (drain,), (update_range,),
         (forward_rows, 0), (forward_rows, 1), (wait_all,), (update_core,), (drain_all,)]
     for act, *which in plan:
         with mark("_".join([act.__name__, *map(str, which[:1])])):
@@ -385,7 +422,7 @@
         pltpu.VMEM((rows * n, s // m), BF16), pltpu.VMEM((core_rows, rows * n), BF16), pltpu.VMEM((k, rows * n), BF16),
         dma((m,)), dma((6,)), dma, dma((chips, 2)), dma, dma,
         dma((slots,)), dma((2, m)), dma, dma((count, m)), dma((count,)),
-        dma, dma((2,)), dma((2,)), dma((2 + chips.bit_length() - 1,)), dma((2,)), dma((3,)),
+        dma, dma((2,)), dma((2,)), dma((2 + chips.bit_length() - 1,)), dma((2,)), dma((3,)), dma((2, m - 1)), dma((2, m - 1)),
     ]
     outputs = (
         jax.ShapeDtypeStruct((k, width), F32), jax.ShapeDtypeStruct((rows, l // m), F32),

time: 81.5 us -> 80.9 us (level)
  Pallas kernels: 79.9 us -> 78.8 us
    pallas_call x1, Pallas kernels: 77.6 us -> 76.6 us  [shards(): pl.pallas_call(functools.partial(sketch_kernel, n, m), out_shape=outputs,...]
where the time goes in v4:
time: 80.9 us; the launch traced here: 79.4 us
  Pallas kernels  78.8 us (97%)
    pallas_call x1, Pallas kernels, shards(): pl.pallas_call(functools.partial(sketch_kernel, n, m), out_shape=outputs,...  76.6 us
    pallas_call x1, Pallas kernels, shards(): pl.pallas_call(store_kernel, out_shape=outputs, in_specs=[vmem] * 3, out_...  2.24 us

profile of v4, /device:TPU:11, one launch (start us, length us, event | category | flops | bytes accessed | tf_op | source)
XLA Modules:
  0.0 79.4 jit_solution(8436173751517074930)
XLA Ops:
  0.6 76.6 %sketch.1 = (f32[512,2048]{1,0:T(8,128)S(1)}, f32[128,256]{1,0:T(8,128)S(1)}, f32[256,512]{1,0:T(8,128)S(1)}) custom-call(bf16[128,16384]{1,0:T(8,128)(2,1)} %window.1, bf16[512,128]{1,0:T(8,128)(2,1)} %omega.1, bf16[2048,1024]{1,0:T(8,128)(2,1)} %psi.1, bf16[2048,2048]{1,0:T(8,128)(2,1)} %ups.1, bf16[2048,128]{1,0:T(8,128)(2,1)} %phi.1, ...), custom_call_target="tpu_custom_call" | custom-call | tf_op jit(solution)/shard_map/sketch/pallas_call | solution.py:431
  77.2 2.2 %store.1 = (f32[512,2048]{1,0:T(8,128)}, f32[128,256]{1,0:T(8,128)}, f32[256,512]{1,0:T(8,128)}) custom-call(f32[512,2048]{1,0:T(8,128)S(1)} %get-tuple-element.6.refs_0_, f32[128,256]{1,0:T(8,128)S(1)} %get-tuple-element.7.refs_1_, f32[256,512]{1,0:T(8,128)S(1)} %get-tuple-element.8.refs_2_), custom_call_target="tpu_custom_call" | custom-call | tf_op jit(solution)/shard_map/store/pallas_call | solution.py:441
